TPU v7x, 32 devices: a whole 2x2x4 slice. The times are simulated.
32 devices in a mesh: seq: 16 (over z, x, core), head: 2 (over y).
Axes of the slice: x: 2, y: 2, z: 4, core: 2. Of those that a mesh axis runs over, the one named last changes fastest.
Arguments:
- prompt_queries: bfloat16 [2, 4096, 4096], P('head', 'seq'), may hold values from -6 to 6
- prompt_keys: bfloat16 [2, 4096, 4096], P('head', 'seq'), may hold values from -0.52734375 to 0.52734375
- prompt_values: bfloat16 [2, 4096, 4096], P('head', 'seq'), may hold values from -0.75 to 0.75
- log_gate: float32 [2, 4096, 32], P('head', 'seq'), may hold values from -1 to 0, as said below
- lengths: int32 [2], P('head'), may hold values from 1 to 4096
- out_gain: float32 [32, 128], replicated, may hold values from 0.5 to 1.5
- step_queries: bfloat16 [64, 2, 128], P(('head', 'seq')), may hold values from -6 to 6
- step_keys: bfloat16 [64, 2, 128], P(('head', 'seq')), may hold values from -0.52734375 to 0.52734375
- step_values: bfloat16 [64, 2, 128], P(('head', 'seq')), may hold values from -6 to 6
- step_gates: float32 [64, 2], P(('head', 'seq')), may hold values from -0.7 to -0.05
Outputs:
- prefill_out: bfloat16 [2, 4096, 4096], P('head', 'seq')
- step_out: bfloat16 [64, 2, 128], P(('head', 'seq'))
- cache_state: float32 [64, 128, 128], P(('head', 'seq'))
Inputs may be any that keep to these rules, and one draw needn't show every extreme that they name: `log_gate`: every entry is negative.
All inputs are finite; a program needn't handle non-finite values.
Results may differ from a plain program's by a relative error of at most 0.0049.
Values sent between devices are 32-bit elements; how exact they have to be, the bound alone decides.
A program may use at most 128 MiB of HBM per device.

v0:
```python
import jax
import jax.numpy as jnp
from jax import lax
from jax.sharding import PartitionSpec as P


def carried_in(part, axis, combine, identity, reverse):
    count = lax.axis_size(axis)
    place = lax.axis_index(axis)
    ahead = count - 1 - place if reverse else place
    gathered = jax.tree.map(lambda a: lax.all_gather(a, axis), part)
    state = jax.tree.map(lambda a, e: jnp.zeros_like(a) + jnp.asarray(e, a.dtype), part, identity)

    def one(step, state):
        source = count - 1 - step if reverse else step
        return combine(
            state, jax.tree.map(lambda a: lax.dynamic_index_in_dim(a, source, 0, False), gathered)
        )

    return lax.fori_loop(0, ahead, one, state)


def head_norm(readout, gain_rows):
    power = jnp.mean(readout * readout, axis=-1, keepdims=True)
    return readout * lax.rsqrt(power + 1e-06) * gain_rows


def carry_join(earlier, later):
    return (earlier[0] + later[0], jnp.exp(later[0])[:, :, None, None] * earlier[1] + later[1])


def decay_join(earlier, later):
    return earlier + later


def per_device(
    prompt_queries,
    prompt_keys,
    prompt_values,
    log_gate,
    lengths,
    out_gain,
    step_queries,
    step_keys,
    step_values,
    step_gates,
):
    highest_precision = lax.Precision.HIGHEST
    batch_dev, group_len, width = prompt_queries.shape
    head_count = log_gate.shape[2]
    key_dim = width // head_count
    value_dim = out_gain.shape[1]
    seq_index = lax.axis_index("seq")
    positions = seq_index * group_len + jnp.arange(group_len)
    valid_rows = positions[None, :] < lengths[:, None]
    gates = jnp.where(valid_rows[:, :, None], log_gate, 0.0)
    cumulative_gates = jnp.cumsum(gates, axis=1)
    totals = cumulative_gates[:, -1, :]
    queries = prompt_queries.reshape(batch_dev, group_len, head_count, key_dim)
    keys_kept = jnp.where(valid_rows[:, :, None], prompt_keys, jnp.zeros_like(prompt_keys)).reshape(
        batch_dev, group_len, head_count, key_dim
    )
    values = prompt_values.reshape(batch_dev, group_len, head_count, value_dim)
    decay_scaled_keys = (
        keys_kept.astype(jnp.float32)
        * jnp.exp(totals[:, None, :] - cumulative_gates)[:, :, :, None]
    ).astype(jnp.bfloat16)
    group_local_state = jnp.einsum(
        "bchk,bchv->hbkv", decay_scaled_keys, values, preferred_element_type=jnp.float32
    )
    head_totals = totals.T
    zero_totals = jnp.zeros_like(head_totals)
    earlier_decay, incoming = carried_in(
        (head_totals, group_local_state),
        "seq",
        carry_join,
        (zero_totals, jnp.zeros_like(group_local_state)),
        False,
    )
    scaled_queries = queries.astype(jnp.float32) * jnp.exp(cumulative_gates)[:, :, :, None]
    cross_group_output = jnp.einsum(
        "bchk,hbkv->bchv", scaled_queries, incoming, precision=highest_precision
    )
    scores = jnp.einsum("bchk,bshk->bhcs", queries, keys_kept, preferred_element_type=jnp.float32)
    leading = jnp.transpose(cumulative_gates, (0, 2, 1))
    spread = leading[:, :, :, None] - leading[:, :, None, :]
    causal = jnp.arange(group_len)[:, None] >= jnp.arange(group_len)[None, :]
    weights = (scores * jnp.exp(jnp.where(causal[None, None], spread, -jnp.inf))).astype(
        jnp.bfloat16
    )
    intra_part = jnp.einsum("bhcs,bshv->bchv", weights, values, preferred_element_type=jnp.float32)
    normed = head_norm(cross_group_output + intra_part, out_gain)
    prefill_out = (
        jnp.where(valid_rows[:, :, None, None], normed, 0.0)
        .astype(jnp.bfloat16)
        .reshape(batch_dev, group_len, head_count * value_dim)
    )
    seq_total = lax.axis_size("seq")
    later_decay = carried_in(head_totals, "seq", decay_join, zero_totals, True)
    weighted_state = jnp.exp(later_decay)[:, :, None, None] * group_local_state
    regrouped = lax.all_to_all(weighted_state, "head", split_axis=0, concat_axis=1, tiled=True)
    flat_states = regrouped.reshape(-1, key_dim, value_dim)
    final_state = lax.psum_scatter(flat_states, "seq", scatter_dimension=0, tiled=True)
    pair_count = final_state.shape[0]
    seq_count = batch_dev * lax.axis_size("head")
    first_row = (lax.axis_index("head") * seq_total + seq_index) * pair_count
    row_heads = (first_row + jnp.arange(pair_count)) // seq_count
    one_hot = (row_heads[:, None] == jnp.arange(head_count)[None, :]).astype(jnp.float32)
    gain_rows = jnp.dot(one_hot, out_gain, precision=highest_precision)
    cache_now = final_state
    readouts = []
    for decode_step in range(step_gates.shape[1]):
        key_float = step_keys[:, decode_step].astype(jnp.float32)
        value_wide_float = step_values[:, decode_step].astype(jnp.float32)
        cache_now = (
            jnp.exp(step_gates[:, decode_step])[:, None, None] * cache_now
            + key_float[:, :, None] * value_wide_float[:, None, :]
        )
        reading = jnp.einsum(
            "pk,pkv->pv",
            step_queries[:, decode_step].astype(jnp.float32),
            cache_now,
            precision=highest_precision,
        )
        readouts.append(head_norm(reading, gain_rows).astype(jnp.bfloat16))
    step_out = jnp.stack(readouts, axis=1)
    return (prefill_out, step_out, cache_now)


def solution(mesh):
    return jax.shard_map(
        per_device,
        mesh=mesh,
        in_specs=(
            P("head", "seq", None),
            P("head", "seq", None),
            P("head", "seq", None),
            P("head", "seq", None),
            P("head"),
            P(),
            P(("head", "seq"), None, None),
            P(("head", "seq"), None, None),
            P(("head", "seq"), None, None),
            P(("head", "seq"), None),
        ),
        out_specs=(
            P("head", "seq", None),
            P(("head", "seq"), None, None),
            P(("head", "seq"), None, None),
        ),
        check_vma=False,
    )
```

profile of v0, /device:TPU:27, one launch (start us, length us, event | category | flops | bytes accessed | tf_op | source)
XLA Modules:
  0.0 349.6 jit_solution(15580858675579103379)
XLA Ops:
  12.2 2.5 copy.88
  14.6 4.1 %copy.89 = bf16[1,256,4096]{1,2,0:T(8,128)(2,1)} copy(bf16[1,256,4096]{2,1,0:T(8,128)(2,1)} %param.16) | data formatting | bytes 4194304 | tf_op jit(solution)/shard_map/reshape.19
  18.8 16.9 %all-gather = f32[16,1,32]{2,1,0:T(1,128)S(1)} all-gather(f32[1,1,32]{2,1,0:T(1,128)S(1)} %copy.63), channel_id=2, replica_groups=mesh['seq'=16,'head'=2] {'seq'}, dimensions={0}, use_global_device_ids=true | all-gather | bytes 2176 | tf_op jit(solution)/shard_map/all_gather | solution.py:11
  35.7 2.9 fusion.18
  39.9 27.1 %all_to_all.15 = f32[32,1,128,128]{3,2,1,0:T(8,128)S(1)} all-to-all(f32[32,1,128,128]{3,2,1,0:T(8,128)S(1)} %multiply_bitcast_fusion), channel_id=1, replica_groups=mesh['seq'=16,'head'=2] {'head'}, dimensions={0} | all-to-all | bytes 4194304 | tf_op jit(solution)/shard_map/all_to_all | solution.py:101
  69.3 3.5 %copy.91 = bf16[32,8,32,128]{3,2,1,0:T(8,128)(2,1)} copy(bf16[32,8,32,128]{3,1,2,0:T(8,128)(2,1)} %bitcast.122) | data formatting | bytes 4194304
  73.2 8.4 %fusion.1 = f32[32,256,128]{1,2,0:T(8,128)} fusion(bf16[256,32,128]{0,2,1:T(8,128)(2,1)} %bitcast.115, f32[32,256]{1,0:T(8,128)S(1)} %bitcast_add_fusion.3, pred[256,256]{0,1:T(8,128)(4,1)S(1)} %iota_compare_fusion, bf16[256,32,128]{0,2,1:T(8,128)(2,1)S(1)} %bitcast.113, bf16[256,32,128]{2,1,0:T(8,128)(2,1)} %bitcast.119), kind=kOutput, calls=%fused_computation.5 | convolution fusion | flops 1082130432 | bytes 10584064 | tf_op jit(solution)/shard_map/bhcs,bshv->bchv/dot_general | solution.py:91
  81.6 47.2 %reduce-scatter.2.cloned.1.call-done = f32[2,128,128]{2,1,0:T(8,128)} async-done(((f32[32,128,128]{2,1,0:T(8,128)}), f32[2,128,128]{2,1,0:T(8,128)}) %reduce-scatter.2.cloned.1.call-update) | async-done | bytes 131088 | tf_op jit(solution)/shard_map/reduce_scatter | solution.py:103
  132.3 168.4 %all-gather.4.cloned.1.call-done = f32[512,128,128]{2,1,0:T(8,128)} async-done(((f32[32,128,128]{2,1,0:T(8,128)}), f32[512,128,128]{2,1,0:T(8,128)}) %all-gather.4.cloned.1.call-update) | async-done | bytes 33554448 | tf_op jit(solution)/shard_map/all_gather | solution.py:11
  300.9 30.6 %while.24 = (s32[]{:T(128)}, f32[32,1,128,128]{3,2,1,0:T(8,128)S(1)}, s32[]{:T(128)}, f32[16,32,1]{1,2,0:T(1,128)S(1)}, f32[16,32,1,128,128]{4,3,1,2,0:T(8,128)}, /*index=5*/s32[]{:T(128)}, s32[]{:T(128)}, s32[]{:T(128)}) while((s32[]{:T(128)}, f32[32,1,128,128]{3,2,1,0:T(8,128)S(1)}, s32[]{:T(128)}, f32[16,32,1]{1,2,0:T(1,128)S(1)}, ...), condition=%wide.region_3.4_spmd, body=%wide.region_2.3_spmd.sunk | while | flops 1048581 | bytes 6291967 | solution.py:20
  300.9 2.0 bitcast_add_fusion.6
  303.0 2.0 bitcast_add_fusion.6
  305.0 2.0 bitcast_add_fusion.6
  307.0 2.0 bitcast_add_fusion.6
  309.0 2.0 bitcast_add_fusion.6
  311.1 2.0 bitcast_add_fusion.6
  313.1 2.0 bitcast_add_fusion.6
  315.1 2.0 bitcast_add_fusion.6
  317.1 2.0 bitcast_add_fusion.6
  319.2 2.0 bitcast_add_fusion.6
  321.2 2.0 bitcast_add_fusion.6
  329.3 2.0 bitcast_add_fusion.6
  331.5 7.6 %fusion.3 = (f32[256,32]{0,1:T(8,128)S(1)}, f32[32,128,256]{2,1,0:T(8,128)S(1)}) fusion(f32[32,256,128]{1,2,0:T(8,128)} %fusion.1, f32[256,32]{0,1:T(8,128)S(1)} %bitcast.125, bf16[256,32,128]{2,1,0:T(8,128)(2,1)} %bitcast.120, f32[32,1,128,128]{3,2,1,0:T(8,128)S(1)} %get-tuple-element.103), kind=kOutput, calls=%fused_computation.8 | convolution fusion | flops 1615847424 | bytes 12648448 | tf_op jit(solution)/shard_map/bchk,hbkv->bchv/dot_general | solution.py:81
  339.9 2.9 copy.78
  (78 shorter events, 18.7 us)
Async XLA Ops:
  7.2 121.6 %reduce-scatter.2.cloned.1.call-start = ((), (), s32[]{:S(2)}) async-start(), calls=%async_computation.2 | async-start | bytes 2228224 | tf_op jit(solution)/shard_map/reduce_scatter | solution.py:103
  38.6 1.3 copy-start
  68.5 232.1 %all-gather.4.cloned.1.call-start = ((), (), s32[]{:S(2)}) async-start(), calls=%async_computation.3 | async-start | bytes 35651584 | tf_op jit(solution)/shard_map/all_gather | solution.py:11
  69.3 3.6 %copy-start.5 = (f32[2,2]{1,0:T(2,128)S(1)}, f32[2,2]{1,0:T(2,128)}, u32[]{:S(2)}) copy-start(f32[2,2]{1,0:T(2,128)} %param.23) | copy-start | bytes 52
  69.3 3.8 %copy-start.6 = (bf16[2,2,128]{2,1,0:T(2,128)(2,1)S(1)}, bf16[2,2,128]{2,1,0:T(2,128)(2,1)}, u32[]{:S(2)}) copy-start(bf16[2,2,128]{2,1,0:T(2,128)(2,1)} %param.21) | copy-start | bytes 3076
  69.3 3.8 %copy-start.7 = (bf16[2,2,128]{2,1,0:T(2,128)(2,1)S(1)}, bf16[2,2,128]{2,1,0:T(2,128)(2,1)}, u32[]{:S(2)}) copy-start(bf16[2,2,128]{2,1,0:T(2,128)(2,1)} %param.22) | copy-start | bytes 3076
  69.3 3.8 %copy-start.1 = (bf16[1,256,4096]{1,2,0:T(8,128)(2,1)S(1)}, bf16[1,256,4096]{1,2,0:T(8,128)(2,1)}, u32[]{:S(2)}) copy-start(bf16[1,256,4096]{1,2,0:T(8,128)(2,1)} %copy.88) | copy-start | bytes 6291460
  73.2 56.7 %copy-start.4 = (bf16[2,2,128]{2,1,0:T(2,128)(2,1)S(1)}, bf16[2,2,128]{2,1,0:T(2,128)(2,1)}, u32[]{:S(2)}) copy-start(bf16[2,2,128]{2,1,0:T(2,128)(2,1)} %param.20) | copy-start | bytes 3076
  73.2 58.3 %copy-start.3 = (f32[32,128]{1,0:T(8,128)S(1)}, f32[32,128]{1,0:T(8,128)}, u32[]{:S(2)}) copy-start(f32[32,128]{1,0:T(8,128)} %param.19) | copy-start | bytes 49156
  129.9 171.0 %copy-start.2 = (f32[2,128,128]{2,1,0:T(8,128)}, f32[2,128,128]{2,1,0:T(8,128)S(1)}, u32[]{:S(2)}) copy-start(f32[2,128,128]{2,1,0:T(8,128)S(1)} %multiply_add_fusion) | copy-start | bytes 393220
Sparse Core Ops, SparseCore 0:
  68.6 60.1 reduce-scatter.1
  130.4 170.1 all-gather.3
where the time goes:
time: 350 us
  waiting for transfers between devices  216 us (62%)
  blocking collectives  43.9 us (13%)
  other arithmetic  35.3 us (10%)
  matrix products  20.5 us (6%)
  local copies, waits for them, and re-layouts  17.7 us (5%)
  between operations  15 us (4%)
    all_gather x1, waiting for transfers between devices, carried_in(): gathered = jax.tree.map(lambda a: lax.all_gather(a, axis), part)  168 us
    reduce_scatter x1, waiting for transfers between devices, per_device(): lax.psum_scatter(flat_states, 'seq', scatter_dimension=0, tiled=True)  47.2 us
    add x15, other arithmetic, carry_join(): jnp.exp(later[0])[:, :, None, None] * earlier[1] + later[1]  29.6 us
    all_to_all x1, blocking collectives, per_device(): lax.all_to_all(weighted_state, 'head', split_axis=0, concat_axis=1, tiled...  27.1 us
    all_gather x1, blocking collectives, carried_in(): gathered = jax.tree.map(lambda a: lax.all_gather(a, axis), part)  16.9 us
    dot_general x1, matrix products, per_device(): jnp.einsum('bhcs,bshv->bchv', weights, values, preferred_element_type=jnp...  8.38 us
    unnamed x21, local copies, waits for them, and re-layouts  8.1 us
    dot_general x1, matrix products, per_device(): jnp.einsum('bchk,hbkv->bchv', scaled_queries, incoming, precision=highest...  7.65 us
  transfers between devices with their start and end apart: 2, of which 2 were waited for; matrix products, arithmetic and copies ran while one was open for 4% of the time, Pallas kernels for 0%

commit v1 on v0

v1 whole, which is shorter than its diff:
```python
import functools
import jax
import jax.numpy as jnp
from jax import lax
from jax.experimental import pallas as pl
from jax.experimental.pallas import tpu as pltpu
from jax.sharding import PartitionSpec as P

MESH = pl.DeviceIdType.MESH
F32 = jnp.float32
BF16 = jnp.bfloat16
LAG = 3
CHUNK = 4


def column(ref, h):
    wide = ref[...]
    lane = lax.broadcasted_iota(jnp.int32, wide.shape, 1)
    return jnp.sum(jnp.where(lane == h, wide, 0.0), axis=1, keepdims=True)


def head_norm(readout, gain_row):
    power = jnp.mean(readout * readout, axis=-1, keepdims=True)
    return readout * lax.rsqrt(power + 1e-06) * gain_row


def kernel(
    n_seq, n_head,
    len_ref, sgate_ref, q_hbm, k_hbm, v_hbm, gate_ref, gain_ref, sq_ref, sk_ref, sv_ref,
    out_hbm, step_ref, cache_ref,
    q_vm, k_vm, v_vm, o_vm, cum, cum_t, dec, a_own, a_oth, x_own, x_nbr, p_in, p_out,
    i_own, i_oth, i_rcv, fin,
    load_sem, out_sem, dec_s, dec_r, a_s, a_r, x_s, x_r, z_s, z_r, i_s, i_r, f_s, f_r,
):
    group = k_vm.shape[0]
    heads = gate_ref.shape[2]
    half = heads // 2
    kd = k_vm.shape[1] // heads
    vd = v_vm.shape[1] // heads
    rows = fin.shape[0]
    seq = lax.axis_index("seq")
    hd = lax.axis_index("head")
    planes = n_seq // 4
    core = seq % 2
    xx = (seq // 2) % 2
    zz = seq // 4
    place = seq % 4
    base = seq - place
    mate = base + 2 * xx + (1 - core)
    across = base + 2 * (1 - xx) + core
    diagonal = base + 2 * (1 - xx) + (1 - core)
    own0 = core * half
    oth0 = (1 - core) * half

    def owner_of(i):
        row = (own0 + i) * n_head + hd
        dev = row // rows
        return dev // n_seq, dev % n_seq, row % rows

    def source_of(p):
        row = (hd * n_seq + seq) * rows + p
        h = row // n_head
        s = (planes - 1) * 4 + ((h % half) % 2) * 2 + h // half
        return s, row % n_head, h

    def loads(h, which):
        width = CHUNK * kd
        at = pl.ds(pl.multiple_of(h * kd, width), width)
        c = h // CHUNK
        src, dst = ((k_hbm, k_vm), (v_hbm, v_vm), (q_hbm, q_vm))[which]
        return pltpu.make_async_copy(src.at[0, :, at], dst.at[:, at], load_sem.at[which, c])

    for c in range(half // CHUNK):
        for first in (oth0, own0):
            loads(first + c * CHUNK, 0).start()
            loads(first + c * CHUNK, 1).start()
    for c in range(half // CHUNK):
        for first in (oth0, own0):
            loads(first + c * CHUNK, 2).start()

    barrier = pltpu.get_barrier_semaphore()
    for other in (mate, across, diagonal):
        pl.semaphore_signal(barrier, inc=1, device_id={"seq": other, "head": hd}, device_id_type=MESH)

    @pl.when(zz > 0)
    def _():
        pl.semaphore_signal(barrier, inc=1, device_id={"seq": seq - 4, "head": hd}, device_id_type=MESH)

    for p in range(rows):
        s, b, _h = source_of(p)

        @pl.when(jnp.logical_or(s != seq, b != hd))
        def _():
            pl.semaphore_signal(barrier, inc=1, device_id={"seq": s, "head": b}, device_id_type=MESH)

    start = seq * group
    length = len_ref[0]
    valid_col = (lax.broadcasted_iota(jnp.int32, (group, 1), 0) + start) < length
    t_iota = lax.broadcasted_iota(jnp.int32, (group, group), 0)
    s_iota = lax.broadcasted_iota(jnp.int32, (group, group), 1)
    gates = jnp.where(valid_col, gate_ref[0], 0.0)
    tril = (t_iota >= s_iota).astype(F32)
    cumulative = jnp.dot(tril, gates, precision=lax.Precision.HIGHEST, preferred_element_type=F32)
    cum[...] = cumulative
    turned = cumulative.T
    cum_t[...] = turned
    dec[place] = jnp.exp(jnp.broadcast_to(turned[:, group - 1:group], (heads, vd)))

    @pl.when(zz == 0)
    def _():
        p_in[...] = jnp.zeros_like(p_in)

    last = zz == planes - 1
    greeted = 0
    for i in range(half):
        oh, os_, _slot = owner_of(i)
        sends = jnp.logical_and(xx == i % 2, jnp.logical_or(oh != hd, os_ != seq))
        greeted = greeted + jnp.where(sends, 1, 0)
    pl.semaphore_wait(barrier, 3 + jnp.where(last, greeted, 1))

    def dec_copy(n, other):
        return pltpu.make_async_remote_copy(
            src_ref=dec.at[place], dst_ref=dec.at[place], send_sem=dec_s.at[n],
            recv_sem=dec_r.at[place], device_id={"seq": other, "head": hd}, device_id_type=MESH)

    def dec_arrival(other):
        slot = other % 4
        return pltpu.make_async_remote_copy(
            src_ref=dec.at[slot], dst_ref=dec.at[slot], send_sem=dec_s.at[0],
            recv_sem=dec_r.at[slot], device_id={"seq": other, "head": hd}, device_id_type=MESH)

    for n, other in enumerate((mate, across, diagonal)):
        dec_copy(n, other).start()

    def send(src, dst, ssem, rsem, s, h=None):
        return pltpu.make_async_remote_copy(
            src_ref=src, dst_ref=dst, send_sem=ssem, recv_sem=rsem,
            device_id={"seq": s, "head": hd if h is None else h}, device_id_type=MESH)

    def a_copy(i):
        return send(a_own.at[oth0 + i], a_oth.at[i], a_s.at[i], a_r.at[i], mate)

    def x_copy(i):
        return send(x_own.at[i], x_nbr.at[i], x_s.at[i], x_r.at[i], across)

    def z_copy(i):
        return send(p_out.at[i], p_in.at[i], z_s.at[i], z_r.at[i], jnp.minimum(seq + 4, n_seq - 4 + place))

    def i_copy(i):
        return send(i_oth.at[i], i_rcv.at[i], i_s.at[i], i_r.at[i], mate)

    def f_copy(i):
        oh, os_, slot = owner_of(i)
        return send(p_out.at[i], fin.at[slot], f_s.at[i], f_r.at[slot], os_, oh)

    def lanes(h):
        return pl.ds(pl.multiple_of(h * kd, kd), kd)

    def local_state(h):
        col = column(cum, h)
        scale = jnp.where(valid_col, jnp.exp(col[group - 1:group, :] - col), 0.0)
        wk = (k_vm[:, lanes(h)].astype(F32) * scale).astype(BF16)
        a_own[h] = lax.dot_general(
            wk, v_vm[:, lanes(h)], (((0,), (0,)), ((), ())), preferred_element_type=F32)

    def wait_loads(i, which):
        @pl.when(i % CHUNK == 0)
        def _():
            c = i // CHUNK * CHUNK
            for w in which:
                loads(oth0 + c, w).wait()
                loads(own0 + c, w).wait()

    def produce(i):
        wait_loads(i, (0, 1))
        local_state(oth0 + i)
        a_copy(i).start()
        local_state(own0 + i)

    def chip_parts(i):
        h = own0 + i
        mine, theirs = a_own[h], a_oth[i]
        early = jnp.where(core == 0, mine, theirs)
        late = jnp.where(core == 0, theirs, mine)
        return early, late

    def combine(i):
        h = own0 + i
        a_copy(i).wait_recv()
        early, late = chip_parts(i)
        x_own[i] = early * dec[2 * xx + 1, pl.ds(h, 1), :] + late
        x_copy(i).start()

    def loop(lo, hi, body):
        def step(i, c):
            body(i)
            return c
        lax.fori_loop(lo, hi, step, 0)

    loop(0, LAG, produce)
    for other in (mate, across, diagonal):
        dec_arrival(other).wait_recv()

    def both(i):
        produce(i)
        combine(i - LAG)

    loop(LAG, half, both)
    loop(half - LAG, half, combine)

    def chain(i):
        h = own0 + i
        x_copy(i).wait_recv()

        @pl.when(zz > 0)
        def _():
            z_copy(i).wait_recv()

        first = xx == 0
        mine, theirs = x_own[i], x_nbr[i]
        d0 = dec[0, pl.ds(h, 1), :] * dec[1, pl.ds(h, 1), :]
        d1 = dec[2, pl.ds(h, 1), :] * dec[3, pl.ds(h, 1), :]
        entering = p_in[i]
        middle = entering * d0 + jnp.where(first, mine, theirs)
        p_out[i] = middle * d1 + jnp.where(first, theirs, mine)

        @pl.when(zz < planes - 1)
        def _():
            z_copy(i).start()

        @pl.when(jnp.logical_and(zz == planes - 1, xx == i % 2))
        def _():
            oh, os_, slot = owner_of(i)
            away = jnp.logical_or(oh != hd, os_ != seq)

            @pl.when(away)
            def _():
                f_copy(i).start()

            @pl.when(jnp.logical_not(away))
            def _():
                fin[slot] = p_out[i]

        early, _late = chip_parts(i)
        into0 = jnp.where(first, entering, middle)
        into1 = into0 * dec[2 * xx, pl.ds(h, 1), :] + early
        i_oth[i] = jnp.where(core == 0, into1, into0)
        i_copy(i).start()
        i_own[i] = jnp.where(core == 0, into0, into1)

    valid_row = (lax.broadcasted_iota(jnp.int32, (1, group), 1) + start) < length

    def out_copy(h):
        return pltpu.make_async_copy(o_vm.at[:, lanes(h)], out_hbm.at[0, :, lanes(h)], out_sem.at[h])

    def head_out(h, state):
        q = q_vm[:, lanes(h)]
        scores = lax.dot_general(
            q, k_vm[:, lanes(h)], (((1,), (1,)), ((), ())), preferred_element_type=F32)
        col = column(cum, h)
        spread = col - cum_t[pl.ds(h, 1), :]
        t_pos = lax.broadcasted_iota(jnp.int32, (group, group), 0)
        s_pos = lax.broadcasted_iota(jnp.int32, (group, group), 1)
        keep = jnp.logical_and(t_pos >= s_pos, valid_row)
        weights = (scores * jnp.exp(jnp.where(keep, spread, -jnp.inf))).astype(BF16)
        intra = jnp.dot(weights, v_vm[:, lanes(h)], preferred_element_type=F32)
        inter = jnp.exp(col) * jnp.dot(q, state.astype(BF16), preferred_element_type=F32)
        normed = head_norm(inter + intra, gain_ref[pl.ds(h, 1), :])
        o_vm[:, lanes(h)] = jnp.where(valid_col, normed, 0.0).astype(BF16)
        out_copy(h).start()

    def other_out(i):
        i_copy(i).wait_recv()
        head_out(oth0 + i, i_rcv[i])

    def first_round(i):
        wait_loads(i, (2,))
        chain(i)
        head_out(own0 + i, i_own[i])

    def later_round(i):
        first_round(i)
        other_out(i - 1)

    loop(0, 1, first_round)
    loop(1, half, later_round)
    other_out(half - 1)

    for p in range(rows):
        s, b, h = source_of(p)

        @pl.when(jnp.logical_or(s != seq, b != hd))
        def _():
            send(fin.at[p], fin.at[p], f_s.at[0], f_r.at[p], s, b).wait_recv()

        gain_row = gain_ref[pl.ds(h, 1), :]
        sk, sv, sq = sk_ref[p].astype(F32), sv_ref[p].astype(F32), sq_ref[p].astype(F32)
        now = fin[p]
        outs = []
        for j in range(sk.shape[0]):
            kcol = jnp.broadcast_to(sk[j:j + 1, :], (vd, kd)).T
            qcol = jnp.broadcast_to(sq[j:j + 1, :], (vd, kd)).T
            now = jnp.exp(jnp.full((1, vd), sgate_ref[p, j], F32)) * now + kcol * sv[j:j + 1, :]
            outs.append(head_norm(jnp.sum(qcol * now, axis=0, keepdims=True), gain_row))
        step_ref[p] = jnp.concatenate(outs, axis=0).astype(BF16)
        cache_ref[p] = now

    for n, other in enumerate((mate, across, diagonal)):
        dec_copy(n, other).wait_send()

    def drain(i):
        a_copy(i).wait_send()
        x_copy(i).wait_send()
        i_copy(i).wait_send()
        out_copy(own0 + i).wait()
        out_copy(oth0 + i).wait()

        @pl.when(zz < planes - 1)
        def _():
            z_copy(i).wait_send()

        @pl.when(jnp.logical_and(zz == planes - 1, xx == i % 2))
        def _():
            oh, os_, _slot = owner_of(i)

            @pl.when(jnp.logical_or(oh != hd, os_ != seq))
            def _():
                f_copy(i).wait_send()

    loop(0, half, drain)


def per_device(n_seq, n_head, pq, pk, pv, lg, ln, gain, sq, sk, sv, sg):
    batch, group, width = pq.shape
    assert batch == 1 and n_seq % 4 == 0
    heads = lg.shape[2]
    half = heads // 2
    kd = width // heads
    vd = gain.shape[1]
    rows = sq.shape[0]
    vm = pl.BlockSpec(memory_space=pltpu.VMEM)
    sm = pl.BlockSpec(memory_space=pltpu.SMEM)
    anyw = pl.BlockSpec(memory_space=pl.ANY)
    state = lambda n: pltpu.VMEM((n, kd, vd), F32)
    dma = lambda *n: pltpu.SemaphoreType.DMA(n)
    return pl.pallas_call(
        functools.partial(kernel, n_seq, n_head),
        out_shape=(
            jax.ShapeDtypeStruct((batch, group, heads * vd), BF16),
            jax.ShapeDtypeStruct(sv.shape, BF16),
            jax.ShapeDtypeStruct((rows, kd, vd), F32),
        ),
        in_specs=[sm, sm, anyw, anyw, anyw, vm, vm, vm, vm, vm],
        out_specs=(anyw, vm, vm),
        scratch_shapes=[
            pltpu.VMEM((group, width), BF16),
            pltpu.VMEM((group, width), BF16),
            pltpu.VMEM((group, heads * vd), BF16),
            pltpu.VMEM((group, heads * vd), BF16),
            pltpu.VMEM((group, heads), F32),
            pltpu.VMEM((heads, group), F32),
            pltpu.VMEM((4, heads, vd), F32),
            state(heads), state(half), state(half), state(half), state(half), state(half),
            state(half), state(half), state(half), state(rows),
            dma(3, heads // CHUNK), dma(heads), dma(3), dma(4),
            dma(half), dma(half), dma(half), dma(half), dma(half), dma(half),
            dma(half), dma(half), dma(half), dma(rows),
        ],
        compiler_params=pltpu.CompilerParams(
            collective_id=0, has_side_effects=True, vmem_limit_bytes=48 * 1024 * 1024),
    )(ln, sg, pq, pk, pv, lg, gain, sq, sk, sv)


def solution(mesh):
    return jax.shard_map(
        functools.partial(per_device, mesh.shape["seq"], mesh.shape["head"]),
        mesh=mesh,
        in_specs=(
            P("head", "seq", None),
            P("head", "seq", None),
            P("head", "seq", None),
            P("head", "seq", None),
            P("head"),
            P(),
            P(("head", "seq"), None, None),
            P(("head", "seq"), None, None),
            P(("head", "seq"), None, None),
            P(("head", "seq"), None),
        ),
        out_specs=(
            P("head", "seq", None),
            P(("head", "seq"), None, None),
            P(("head", "seq"), None, None),
        ),
        check_vma=False,
    )
```

time: 350 us -> 61.6 us (0.18)
  waiting for transfers between devices: 216 us -> 0 us
  Pallas kernels: 0 us -> 51.5 us
  blocking collectives: 43.9 us -> 0 us
  other arithmetic: 35.3 us -> 0 us
  matrix products: 20.5 us -> 0 us
  between operations: 15 us -> 1.3 us
  local copies, waits for them, and re-layouts: 17.7 us -> 8.41 us
    all_gather x1 -> x0, waiting for transfers between devices: 168 us -> none  [carried_in(): gathered = jax.tree.map(lambda a: lax.all_gather(a, axis), part)]
    pallas_call x0 -> x1, Pallas kernels: none -> 51.5 us  [per_device(): pl.pallas_call(functools.partial(kernel, n_seq, n_head), out_shape=(jax.S...]
    reduce_scatter x1 -> x0, waiting for transfers between devices: 47.2 us -> none  [per_device(): lax.psum_scatter(flat_states, 'seq', scatter_dimension=0, tiled=True)]
    add x16 -> x0, other arithmetic: 30.7 us -> none  [the longest x15 29.6 us: carry_join(): jnp.exp(later[0])[:, :, None, None] * earlier[1] + later[1]]
    all_to_all x1 -> x0, blocking collectives: 27.1 us -> none  [per_device(): lax.all_to_all(weighted_state, 'head', split_axis=0, concat_axis=1, tiled...]
    dot_general x6 -> x0, matrix products: 20.5 us -> none  [the longest x1 8.38 us: per_device(): jnp.einsum('bhcs,bshv->bchv', weights, values, preferred_element_type=jnp...]
    all_gather x1 -> x0, blocking collectives: 16.9 us -> none  [carried_in(): gathered = jax.tree.map(lambda a: lax.all_gather(a, axis), part)]
    another operation x6 -> x0, local copies, waits for them, and re-layouts: 4.31 us -> none
  transfers between devices with their start and end apart: 2 -> 0, of which waited for: 2 -> 0; matrix products, arithmetic and copies ran while one was open for 4% -> 0% of each run, Pallas kernels for 0% -> 0%
where the time goes in v1:
time: 61.6 us; the launch traced here: 61.2 us
  Pallas kernels  51.5 us (84%)
  local copies, waits for them, and re-layouts  8.41 us (14%)
  between operations  1.3 us (2%)
    pallas_call x1, Pallas kernels, per_device(): pl.pallas_call(functools.partial(kernel, n_seq, n_head), out_shape=(jax.S...  51.5 us
    unnamed x16, local copies, waits for them, and re-layouts  8.41 us

profile of v1, /device:TPU:27, one launch (start us, length us, event | category | flops | bytes accessed | tf_op | source)
XLA Modules:
  0.0 61.2 jit_solution(16219400774984966935)
XLA Ops:
  1.3 0.9 %copy.13.gate_ref = f32[1,256,32]{2,1,0:T(8,128)S(1)} copy(f32[1,256,32]{1,2,0:T(8,128)} %param.13) | data formatting | bytes 65536 | tf_op args[3]
  2.1 0.0 copy-start
  2.1 1.6 %copy-done = bf16[1,256,4096]{2,1,0:T(8,128)(2,1)S(1)} copy-done((bf16[1,256,4096]{2,1,0:T(8,128)(2,1)S(1)}, bf16[1,256,4096]{2,1,0:T(8,128)(2,1)}, u32[]{:S(2)}) %copy-start) | copy-done | bytes 2097176
  3.7 0.0 copy-start.1
  3.7 0.7 %copy-done.1 = f32[32,128]{1,0:T(8,128)S(1)} copy-done((f32[32,128]{1,0:T(8,128)S(1)}, f32[32,128]{1,0:T(8,128)}, u32[]{:S(2)}) %copy-start.1) | copy-done | bytes 16408
  4.4 0.0 copy-start.2
  4.4 0.7 %copy-done.2 = f32[2,2]{1,0:T(2,128)S(1)} copy-done((f32[2,2]{1,0:T(2,128)S(1)}, f32[2,2]{1,0:T(2,128)}, u32[]{:S(2)}) %copy-start.2) | copy-done | bytes 40
  5.1 0.0 copy-start.3
  5.1 0.7 %copy-done.3 = bf16[2,2,128]{2,1,0:T(2,128)(2,1)S(1)} copy-done((bf16[2,2,128]{2,1,0:T(2,128)(2,1)S(1)}, bf16[2,2,128]{2,1,0:T(2,128)(2,1)}, u32[]{:S(2)}) %copy-start.3) | copy-done | bytes 1048
  5.8 0.0 copy-start.4
  5.8 0.7 %copy-done.4 = bf16[2,2,128]{2,1,0:T(2,128)(2,1)S(1)} copy-done((bf16[2,2,128]{2,1,0:T(2,128)(2,1)S(1)}, bf16[2,2,128]{2,1,0:T(2,128)(2,1)}, u32[]{:S(2)}) %copy-start.4) | copy-done | bytes 1048
  6.5 0.0 copy-start.5
  6.5 0.7 %copy-done.5 = bf16[2,2,128]{2,1,0:T(2,128)(2,1)S(1)} copy-done((bf16[2,2,128]{2,1,0:T(2,128)(2,1)S(1)}, bf16[2,2,128]{2,1,0:T(2,128)(2,1)}, u32[]{:S(2)}) %copy-start.5) | copy-done | bytes 1048
  7.2 51.5 %shard_map.121 = (bf16[1,256,4096]{2,1,0:T(8,128)(2,1)S(1)}, bf16[2,2,128]{2,1,0:T(2,128)(2,1)S(1)}, f32[2,128,128]{2,1,0:T(8,128)S(1)}) custom-call(s32[1]{0:T(128)S(6)} %copy.17.len_ref, f32[2,2]{1,0:T(2,128)S(1)} %copy-done.2, bf16[1,256,4096]{2,1,0:T(8,128)(2,1)S(1)} %copy-done, bf16[1,256,4096]{2,1,0:T(8,128)(2,1)} %k_hbm.1, ...), custom_call_target="tpu_custom_call" | custom-call | tf_op jit(solution)/shard_map/pallas_call | solution.py:346
  58.7 1.3 %copy.18 = bf16[1,256,4096]{2,1,0:T(8,128)(2,1)} copy(bf16[1,256,4096]{2,1,0:T(8,128)(2,1)S(1)} %get-tuple-element.6) | data formatting | bytes 4194304
  60.0 0.6 copy.19
  60.6 0.7 %copy.20 = f32[2,128,128]{2,1,0:T(8,128)} copy(f32[2,128,128]{2,1,0:T(8,128)S(1)} %get-tuple-element.8) | data formatting | bytes 262144
Async XLA Ops:
  2.1 1.6 %copy-start = (bf16[1,256,4096]{2,1,0:T(8,128)(2,1)S(1)}, bf16[1,256,4096]{2,1,0:T(8,128)(2,1)}, u32[]{:S(2)}) copy-start(bf16[1,256,4096]{2,1,0:T(8,128)(2,1)} %q_hbm.1) | copy-start | bytes 6291460
  3.7 0.7 %copy-start.1 = (f32[32,128]{1,0:T(8,128)S(1)}, f32[32,128]{1,0:T(8,128)}, u32[]{:S(2)}) copy-start(f32[32,128]{1,0:T(8,128)} %gain_ref.1) | copy-start | bytes 49156
  4.4 0.7 %copy-start.2 = (f32[2,2]{1,0:T(2,128)S(1)}, f32[2,2]{1,0:T(2,128)}, u32[]{:S(2)}) copy-start(f32[2,2]{1,0:T(2,128)} %sgate_ref.1) | copy-start | bytes 52
  5.1 0.7 %copy-start.3 = (bf16[2,2,128]{2,1,0:T(2,128)(2,1)S(1)}, bf16[2,2,128]{2,1,0:T(2,128)(2,1)}, u32[]{:S(2)}) copy-start(bf16[2,2,128]{2,1,0:T(2,128)(2,1)} %sq_ref.1) | copy-start | bytes 3076
  5.8 0.7 %copy-start.4 = (bf16[2,2,128]{2,1,0:T(2,128)(2,1)S(1)}, bf16[2,2,128]{2,1,0:T(2,128)(2,1)}, u32[]{:S(2)}) copy-start(bf16[2,2,128]{2,1,0:T(2,128)(2,1)} %sk_ref.1) | copy-start | bytes 3076
  6.5 0.7 %copy-start.5 = (bf16[2,2,128]{2,1,0:T(2,128)(2,1)S(1)}, bf16[2,2,128]{2,1,0:T(2,128)(2,1)}, u32[]{:S(2)}) copy-start(bf16[2,2,128]{2,1,0:T(2,128)(2,1)} %sv_ref.1) | copy-start | bytes 3076

commit v2 on v1

--- a/solution.py
+++ b/solution.py
@@ -9,7 +9,7 @@
 MESH = pl.DeviceIdType.MESH
 F32 = jnp.float32
 BF16 = jnp.bfloat16
-LAG = 3
+LAG = 2
 CHUNK = 4
 
 
@@ -26,14 +26,14 @@
 
 def kernel(
     n_seq, n_head,
-    len_ref, sgate_ref, q_hbm, k_hbm, v_hbm, gate_ref, gain_ref, sq_ref, sk_ref, sv_ref,
-    out_hbm, step_ref, cache_ref,
-    q_vm, k_vm, v_vm, o_vm, cum, cum_t, dec, a_own, a_oth, x_own, x_nbr, p_in, p_out,
+    len_ref, q_hbm, k_hbm, v_hbm, gate_hbm, gain_hbm, sq_hbm, sk_hbm, sv_hbm, sg_hbm,
+    o_vm, step_ref, cache_ref,
+    q_vm, k_vm, v_vm, gate_ref, gain_ref, sq_ref, sk_ref, sv_ref, sgate_ref, intra, cum, cum_t, dec, a_own, a_oth, x_own, x_nbr, p_in, p_out,
     i_own, i_oth, i_rcv, fin,
-    load_sem, out_sem, dec_s, dec_r, a_s, a_r, x_s, x_r, z_s, z_r, i_s, i_r, f_s, f_r,
+    load_sem, small_sem, dec_s, dec_r, a_s, a_r, x_s, x_r, z_s, z_r, i_s, i_r, f_s, f_r,
 ):
     group = k_vm.shape[0]
-    heads = gate_ref.shape[2]
+    heads = gate_ref.shape[1]
     half = heads // 2
     kd = k_vm.shape[1] // heads
     vd = v_vm.shape[1] // heads
@@ -70,6 +70,14 @@
         src, dst = ((k_hbm, k_vm), (v_hbm, v_vm), (q_hbm, q_vm))[which]
         return pltpu.make_async_copy(src.at[0, :, at], dst.at[:, at], load_sem.at[which, c])
 
+    small = [
+        pltpu.make_async_copy(src, dst, small_sem.at[n])
+        for n, (src, dst) in enumerate((
+            (gate_hbm, gate_ref), (gain_hbm, gain_ref), (sq_hbm, sq_ref), (sk_hbm, sk_ref),
+            (sv_hbm, sv_ref), (sg_hbm, sgate_ref)))
+    ]
+    for copy in small:
+        copy.start()
     for c in range(half // CHUNK):
         for first in (oth0, own0):
             loads(first + c * CHUNK, 0).start()
@@ -98,12 +106,13 @@
     valid_col = (lax.broadcasted_iota(jnp.int32, (group, 1), 0) + start) < length
     t_iota = lax.broadcasted_iota(jnp.int32, (group, group), 0)
     s_iota = lax.broadcasted_iota(jnp.int32, (group, group), 1)
-    gates = jnp.where(valid_col, gate_ref[0], 0.0)
-    tril = (t_iota >= s_iota).astype(F32)
-    cumulative = jnp.dot(tril, gates, precision=lax.Precision.HIGHEST, preferred_element_type=F32)
-    cum[...] = cumulative
-    turned = cumulative.T
+    valid_row = (lax.broadcasted_iota(jnp.int32, (1, group), 1) + start) < length
+    small[0].wait()
+    gates = jnp.where(valid_row, gate_ref[0], 0.0)
+    triu = (t_iota <= s_iota).astype(F32)
+    turned = jnp.dot(gates, triu, precision=lax.Precision.HIGHEST, preferred_element_type=F32)
     cum_t[...] = turned
+    cum[...] = turned.T
     dec[place] = jnp.exp(jnp.broadcast_to(turned[:, group - 1:group], (heads, vd)))
 
     @pl.when(zz == 0)
@@ -140,11 +149,17 @@
     def a_copy(i):
         return send(a_own.at[oth0 + i], a_oth.at[i], a_s.at[i], a_r.at[i], mate)
 
-    def x_copy(i):
-        return send(x_own.at[i], x_nbr.at[i], x_s.at[i], x_r.at[i], across)
-
-    def z_copy(i):
-        return send(p_out.at[i], p_in.at[i], z_s.at[i], z_r.at[i], jnp.minimum(seq + 4, n_seq - 4 + place))
+    def part(r):
+        return pl.ds(r * (kd // 2), kd // 2)
+
+    def x_copy(i, r):
+        n = 2 * i + r
+        return send(x_own.at[i, part(r)], x_nbr.at[i, part(r)], x_s.at[n], x_r.at[n], across)
+
+    def z_copy(i, r):
+        n = 2 * i + r
+        return send(p_out.at[i, part(r)], p_in.at[i, part(r)], z_s.at[n], z_r.at[n],
+                    jnp.minimum(seq + 4, n_seq - 4 + place))
 
     def i_copy(i):
         return send(i_oth.at[i], i_rcv.at[i], i_s.at[i], i_r.at[i], mate)
@@ -160,7 +175,7 @@
         col = column(cum, h)
         scale = jnp.where(valid_col, jnp.exp(col[group - 1:group, :] - col), 0.0)
         wk = (k_vm[:, lanes(h)].astype(F32) * scale).astype(BF16)
-        a_own[h] = lax.dot_general(
+        return lax.dot_general(
             wk, v_vm[:, lanes(h)], (((0,), (0,)), ((), ())), preferred_element_type=F32)
 
     def wait_loads(i, which):
@@ -173,118 +188,140 @@
 
     def produce(i):
         wait_loads(i, (0, 1))
-        local_state(oth0 + i)
+        one, two = local_state(oth0 + i), local_state(own0 + i)
+        a_own[oth0 + i] = one
         a_copy(i).start()
-        local_state(own0 + i)
-
-    def chip_parts(i):
+        a_own[own0 + i] = two
+
+    def combine(i):
         h = own0 + i
+        a_copy(i).wait_recv()
         mine, theirs = a_own[h], a_oth[i]
         early = jnp.where(core == 0, mine, theirs)
         late = jnp.where(core == 0, theirs, mine)
-        return early, late
-
-    def combine(i):
+        x_own[i] = early * dec[2 * xx + 1, pl.ds(h, 1), :] + late
+        for r in range(2):
+            x_copy(i, r).start()
+
+    def chain(i, r):
         h = own0 + i
-        a_copy(i).wait_recv()
-        early, late = chip_parts(i)
-        x_own[i] = early * dec[2 * xx + 1, pl.ds(h, 1), :] + late
-        x_copy(i).start()
-
-    def loop(lo, hi, body):
-        def step(i, c):
-            body(i)
-            return c
-        lax.fori_loop(lo, hi, step, 0)
-
-    loop(0, LAG, produce)
-    for other in (mate, across, diagonal):
-        dec_arrival(other).wait_recv()
-
-    def both(i):
-        produce(i)
-        combine(i - LAG)
-
-    loop(LAG, half, both)
-    loop(half - LAG, half, combine)
-
-    def chain(i):
-        h = own0 + i
-        x_copy(i).wait_recv()
+        x_copy(i, r).wait_recv()
 
         @pl.when(zz > 0)
         def _():
-            z_copy(i).wait_recv()
+            z_copy(i, r).wait_recv()
 
         first = xx == 0
-        mine, theirs = x_own[i], x_nbr[i]
+        at = part(r)
+        mine, theirs = x_own[i, at], x_nbr[i, at]
         d0 = dec[0, pl.ds(h, 1), :] * dec[1, pl.ds(h, 1), :]
         d1 = dec[2, pl.ds(h, 1), :] * dec[3, pl.ds(h, 1), :]
-        entering = p_in[i]
+        entering = p_in[i, at]
         middle = entering * d0 + jnp.where(first, mine, theirs)
-        p_out[i] = middle * d1 + jnp.where(first, theirs, mine)
+        p_out[i, at] = middle * d1 + jnp.where(first, theirs, mine)
 
         @pl.when(zz < planes - 1)
         def _():
-            z_copy(i).start()
-
-        @pl.when(jnp.logical_and(zz == planes - 1, xx == i % 2))
-        def _():
-            oh, os_, slot = owner_of(i)
-            away = jnp.logical_or(oh != hd, os_ != seq)
-
-            @pl.when(away)
+            z_copy(i, r).start()
+
+        if r == 1:
+            @pl.when(jnp.logical_and(zz == planes - 1, xx == i % 2))
             def _():
-                f_copy(i).start()
-
-            @pl.when(jnp.logical_not(away))
-            def _():
-                fin[slot] = p_out[i]
-
-        early, _late = chip_parts(i)
+                oh, os_, slot = owner_of(i)
+                away = jnp.logical_or(oh != hd, os_ != seq)
+
+                @pl.when(away)
+                def _():
+                    f_copy(i).start()
+
+                @pl.when(jnp.logical_not(away))
+                def _():
+                    fin[slot] = p_out[i]
+
+        early = jnp.where(core == 0, a_own[h, at], a_oth[i, at])
         into0 = jnp.where(first, entering, middle)
         into1 = into0 * dec[2 * xx, pl.ds(h, 1), :] + early
-        i_oth[i] = jnp.where(core == 0, into1, into0)
-        i_copy(i).start()
-        i_own[i] = jnp.where(core == 0, into0, into1)
-
-    valid_row = (lax.broadcasted_iota(jnp.int32, (1, group), 1) + start) < length
-
-    def out_copy(h):
-        return pltpu.make_async_copy(o_vm.at[:, lanes(h)], out_hbm.at[0, :, lanes(h)], out_sem.at[h])
-
-    def head_out(h, state):
-        q = q_vm[:, lanes(h)]
+        i_oth[i, at] = jnp.where(core == 0, into1, into0)
+        if r == 1:
+            i_copy(i).start()
+        i_own[i, at] = jnp.where(core == 0, into0, into1)
+
+    def inside(h):
         scores = lax.dot_general(
-            q, k_vm[:, lanes(h)], (((1,), (1,)), ((), ())), preferred_element_type=F32)
-        col = column(cum, h)
-        spread = col - cum_t[pl.ds(h, 1), :]
+            q_vm[:, lanes(h)], k_vm[:, lanes(h)], (((1,), (1,)), ((), ())),
+            preferred_element_type=F32)
+        spread = column(cum, h) - cum_t[pl.ds(h, 1), :]
         t_pos = lax.broadcasted_iota(jnp.int32, (group, group), 0)
         s_pos = lax.broadcasted_iota(jnp.int32, (group, group), 1)
         keep = jnp.logical_and(t_pos >= s_pos, valid_row)
         weights = (scores * jnp.exp(jnp.where(keep, spread, -jnp.inf))).astype(BF16)
-        intra = jnp.dot(weights, v_vm[:, lanes(h)], preferred_element_type=F32)
-        inter = jnp.exp(col) * jnp.dot(q, state.astype(BF16), preferred_element_type=F32)
-        normed = head_norm(inter + intra, gain_ref[pl.ds(h, 1), :])
-        o_vm[:, lanes(h)] = jnp.where(valid_col, normed, 0.0).astype(BF16)
-        out_copy(h).start()
-
-    def other_out(i):
-        i_copy(i).wait_recv()
-        head_out(oth0 + i, i_rcv[i])
-
-    def first_round(i):
+        return jnp.dot(weights, v_vm[:, lanes(h)], preferred_element_type=F32)
+
+    def inside_pair(i):
         wait_loads(i, (2,))
-        chain(i)
-        head_out(own0 + i, i_own[i])
-
-    def later_round(i):
-        first_round(i)
-        other_out(i - 1)
-
-    loop(0, 1, first_round)
-    loop(1, half, later_round)
-    other_out(half - 1)
+        one, two = inside(own0 + i), inside(oth0 + i)
+        intra[own0 + i] = one
+        intra[oth0 + i] = two
+
+    def finish(h, state):
+        inter = jnp.exp(column(cum, h)) * jnp.dot(
+            q_vm[:, lanes(h)], state.astype(BF16), preferred_element_type=F32)
+        normed = head_norm(inter + intra[h], gain_ref[pl.ds(h, 1), :])
+        return jnp.where(valid_col, normed, 0.0).astype(BF16)
+
+    def put(h, block):
+        o_vm[0, :, lanes(h)] = block
+
+    lag = 4 + 2 * jnp.minimum(zz, 3)
+
+    def round_of(n, c):
+        i = n - lag
+        running = jnp.logical_and(i >= 0, i < half)
+
+        @pl.when(n < half)
+        def _():
+            produce(n)
+
+        @pl.when(n == LAG - 1)
+        def _():
+            for other in (mate, across, diagonal):
+                dec_arrival(other).wait_recv()
+
+        @pl.when(jnp.logical_and(n >= LAG, n < half + LAG))
+        def _():
+            combine(n - LAG)
+
+        @pl.when(running)
+        def _():
+            chain(i, 0)
+
+        @pl.when(n < half)
+        def _():
+            inside_pair(n)
+
+        @pl.when(running)
+        def _():
+            chain(i, 1)
+
+        @pl.when(i == 0)
+        def _():
+            put(own0, finish(own0, i_own[0]))
+
+        @pl.when(jnp.logical_and(i > 0, i < half))
+        def _():
+            i_copy(i - 1).wait_recv()
+            one = finish(own0 + i, i_own[i])
+            two = finish(oth0 + i - 1, i_rcv[i - 1])
+            put(own0 + i, one)
+            put(oth0 + i - 1, two)
+
+        return c
+
+    for copy in small[1:]:
+        copy.wait()
+    lax.fori_loop(0, half + lag, round_of, 0)
+    i_copy(half - 1).wait_recv()
+    put(oth0 + half - 1, finish(oth0 + half - 1, i_rcv[half - 1]))
 
     for p in range(rows):
         s, b, h = source_of(p)
@@ -300,7 +337,7 @@
         for j in range(sk.shape[0]):
             kcol = jnp.broadcast_to(sk[j:j + 1, :], (vd, kd)).T
             qcol = jnp.broadcast_to(sq[j:j + 1, :], (vd, kd)).T
-            now = jnp.exp(jnp.full((1, vd), sgate_ref[p, j], F32)) * now + kcol * sv[j:j + 1, :]
+            now = jnp.exp(jnp.broadcast_to(sgate_ref[p:p + 1, j:j + 1], (1, vd))) * now + kcol * sv[j:j + 1, :]
             outs.append(head_norm(jnp.sum(qcol * now, axis=0, keepdims=True), gain_row))
         step_ref[p] = jnp.concatenate(outs, axis=0).astype(BF16)
         cache_ref[p] = now
@@ -308,16 +345,16 @@
     for n, other in enumerate((mate, across, diagonal)):
         dec_copy(n, other).wait_send()
 
-    def drain(i):
+    def drain(i, c):
         a_copy(i).wait_send()
-        x_copy(i).wait_send()
         i_copy(i).wait_send()
-        out_copy(own0 + i).wait()
-        out_copy(oth0 + i).wait()
+        for r in range(2):
+            x_copy(i, r).wait_send()
 
         @pl.when(zz < planes - 1)
         def _():
-            z_copy(i).wait_send()
+            for r in range(2):
+                z_copy(i, r).wait_send()
 
         @pl.when(jnp.logical_and(zz == planes - 1, xx == i % 2))
         def _():
@@ -327,7 +364,18 @@
             def _():
                 f_copy(i).wait_send()
 
-    loop(0, half, drain)
+        return c
+
+    lax.fori_loop(0, half, drain, 0)
+
+
+def store_kernel(*refs):
+    n = len(refs) // 2
+    copies = [pltpu.make_async_copy(refs[j], refs[n + j], refs[-1].at[j]) for j in range(n)]
+    for copy in copies:
+        copy.start()
+    for copy in copies:
+        copy.wait()
 
 
 def per_device(n_seq, n_head, pq, pk, pv, lg, ln, gain, sq, sk, sv, sg):
@@ -340,35 +388,49 @@
     rows = sq.shape[0]
     vm = pl.BlockSpec(memory_space=pltpu.VMEM)
     sm = pl.BlockSpec(memory_space=pltpu.SMEM)
-    anyw = pl.BlockSpec(memory_space=pl.ANY)
+    far = pl.BlockSpec(memory_space=pltpu.HBM)
     state = lambda n: pltpu.VMEM((n, kd, vd), F32)
     dma = lambda *n: pltpu.SemaphoreType.DMA(n)
-    return pl.pallas_call(
+    results = pl.pallas_call(
         functools.partial(kernel, n_seq, n_head),
         out_shape=(
-            jax.ShapeDtypeStruct((batch, group, heads * vd), BF16),
-            jax.ShapeDtypeStruct(sv.shape, BF16),
-            jax.ShapeDtypeStruct((rows, kd, vd), F32),
+            pltpu.VMEM((batch, group, heads * vd), BF16),
+            pltpu.VMEM(sv.shape, BF16),
+            pltpu.VMEM((rows, kd, vd), F32),
         ),
-        in_specs=[sm, sm, anyw, anyw, anyw, vm, vm, vm, vm, vm],
-        out_specs=(anyw, vm, vm),
+        in_specs=[sm] + [far] * 9,
+        out_specs=(vm, vm, vm),
         scratch_shapes=[
             pltpu.VMEM((group, width), BF16),
             pltpu.VMEM((group, width), BF16),
             pltpu.VMEM((group, heads * vd), BF16),
-            pltpu.VMEM((group, heads * vd), BF16),
+            pltpu.VMEM((batch, heads, group), F32),
+            pltpu.VMEM(gain.shape, F32),
+            pltpu.VMEM(sq.shape, BF16),
+            pltpu.VMEM(sk.shape, BF16),
+            pltpu.VMEM(sv.shape, BF16),
+            pltpu.VMEM(sg.shape, F32),
+            pltpu.VMEM((heads, group, vd), F32),
             pltpu.VMEM((group, heads), F32),
             pltpu.VMEM((heads, group), F32),
             pltpu.VMEM((4, heads, vd), F32),
             state(heads), state(half), state(half), state(half), state(half), state(half),
             state(half), state(half), state(half), state(rows),
-            dma(3, heads // CHUNK), dma(heads), dma(3), dma(4),
-            dma(half), dma(half), dma(half), dma(half), dma(half), dma(half),
+            dma(3, heads // CHUNK), dma(6), dma(3), dma(4),
+            dma(half), dma(half), dma(heads), dma(heads), dma(heads), dma(heads),
             dma(half), dma(half), dma(half), dma(rows),
         ],
         compiler_params=pltpu.CompilerParams(
-            collective_id=0, has_side_effects=True, vmem_limit_bytes=48 * 1024 * 1024),
-    )(ln, sg, pq, pk, pv, lg, gain, sq, sk, sv)
+            collective_id=0, has_side_effects=True, vmem_limit_bytes=60 * 1024 * 1024),
+    )(ln, pq, pk, pv, jnp.transpose(lg, (0, 2, 1)), gain, sq, sk, sv, sg)
+    return pl.pallas_call(
+        store_kernel,
+        out_shape=tuple(jax.ShapeDtypeStruct(r.shape, r.dtype) for r in results),
+        in_specs=[vm] * 3,
+        out_specs=(far,) * 3,
+        scratch_shapes=[dma(3)],
+        compiler_params=pltpu.CompilerParams(vmem_limit_bytes=8 * 1024 * 1024),
+    )(*results)
 
 
 def solution(mesh):

time: 61.6 us -> 50.5 us (0.82)
  local copies, waits for them, and re-layouts: 8.41 us -> 0 us
  Pallas kernels: 51.5 us -> 49.1 us
    unnamed x16 -> x0, local copies, waits for them, and re-layouts: 8.41 us -> none
    pallas_call x1 -> x2, Pallas kernels: 51.5 us -> 49.1 us  [the longest x1 47.7 us: per_device(): pl.pallas_call(functools.partial(kernel, n_seq, n_head), out_shape=(pltpu...]
where the time goes in v2:
time: 50.5 us; the launch traced here: 50.4 us
  Pallas kernels  49.1 us (97%)
  between operations  1.29 us (3%)
    pallas_call x1, Pallas kernels, per_device(): pl.pallas_call(functools.partial(kernel, n_seq, n_head), out_shape=(pltpu...  47.7 us
    pallas_call x1, Pallas kernels, per_device(): pl.pallas_call(store_kernel, out_shape=tuple((jax.ShapeDtypeStruct(r.shap...  1.38 us

profile of v2, /device:TPU:27, one launch (start us, length us, event | category | flops | bytes accessed | tf_op | source)
XLA Modules:
  0.0 50.4 jit_solution(11341685552520944016)
XLA Ops:
  1.3 47.7 %shard_map.121 = (bf16[1,256,4096]{2,1,0:T(8,128)(2,1)S(1)}, bf16[2,2,128]{2,1,0:T(2,128)(2,1)S(1)}, f32[2,128,128]{2,1,0:T(8,128)S(1)}) custom-call(s32[1]{0:T(128)S(6)} %copy.13.len_ref, bf16[1,256,4096]{2,1,0:T(8,128)(2,1)} %q_hbm.1, bf16[1,256,4096]{2,1,0:T(8,128)(2,1)} %k_hbm.1, bf16[1,256,4096]{2,1,0:T(8,128)(2,1)} %v_hbm.1, f32[1,32,256]{2,1,0:T(8,128)} %bitcast.1, ...), custom_call_target="tpu_custom_call" | custom-call | tf_op jit(solution)/shard_map/pallas_call | solution.py:394
  49.0 1.4 %shard_map.122 = (bf16[1,256,4096]{2,1,0:T(8,128)(2,1)}, bf16[2,2,128]{2,1,0:T(2,128)(2,1)}, f32[2,128,128]{2,1,0:T(8,128)}) custom-call(bf16[1,256,4096]{2,1,0:T(8,128)(2,1)S(1)} %get-tuple-element.6.refs_0_, bf16[2,2,128]{2,1,0:T(2,128)(2,1)S(1)} %get-tuple-element.7.refs_1_, f32[2,128,128]{2,1,0:T(8,128)S(1)} %get-tuple-element.8.refs_2_), custom_call_target="tpu_custom_call" | custom-call | tf_op jit(solution)/shard_map/pallas_call | solution.py:426

commit v3 on v2

--- a/solution.py
+++ b/solution.py
@@ -10,6 +10,7 @@
 F32 = jnp.float32
 BF16 = jnp.bfloat16
 LAG = 2
+AHEAD = 3
 CHUNK = 4
 
 
@@ -247,15 +248,21 @@
         i_own[i, at] = jnp.where(core == 0, into0, into1)
 
     def inside(h):
-        scores = lax.dot_general(
-            q_vm[:, lanes(h)], k_vm[:, lanes(h)], (((1,), (1,)), ((), ())),
-            preferred_element_type=F32)
-        spread = column(cum, h) - cum_t[pl.ds(h, 1), :]
-        t_pos = lax.broadcasted_iota(jnp.int32, (group, group), 0)
-        s_pos = lax.broadcasted_iota(jnp.int32, (group, group), 1)
-        keep = jnp.logical_and(t_pos >= s_pos, valid_row)
-        weights = (scores * jnp.exp(jnp.where(keep, spread, -jnp.inf))).astype(BF16)
-        return jnp.dot(weights, v_vm[:, lanes(h)], preferred_element_type=F32)
+        col = column(cum, h)
+        row = cum_t[pl.ds(h, 1), :]
+        blocks = []
+        for lo in (0, group // 2):
+            hi = lo + group // 2
+            scores = lax.dot_general(
+                q_vm[lo:hi, lanes(h)], k_vm[:hi, lanes(h)], (((1,), (1,)), ((), ())),
+                preferred_element_type=F32)
+            spread = col[lo:hi] - row[:, :hi]
+            t_pos = lax.broadcasted_iota(jnp.int32, (hi - lo, hi), 0) + lo
+            s_pos = lax.broadcasted_iota(jnp.int32, (hi - lo, hi), 1)
+            keep = jnp.logical_and(t_pos >= s_pos, valid_row[:, :hi])
+            weights = (scores * jnp.exp(jnp.where(keep, spread, -jnp.inf))).astype(BF16)
+            blocks.append(jnp.dot(weights, v_vm[:hi, lanes(h)], preferred_element_type=F32))
+        return jnp.concatenate(blocks, axis=0)
 
     def inside_pair(i):
         wait_loads(i, (2,))
@@ -295,9 +302,9 @@
         def _():
             chain(i, 0)
 
-        @pl.when(n < half)
-        def _():
-            inside_pair(n)
+        @pl.when(jnp.logical_and(n >= AHEAD, n < half + AHEAD))
+        def _():
+            inside_pair(n - AHEAD)
 
         @pl.when(running)
         def _():

time: 50.5 us -> 50.6 us (level)
  no operation moved by 1% of the time
where the time goes in v3:
time: 50.6 us; the launch traced here: 50.5 us
  Pallas kernels  49.2 us (97%)
  between operations  1.29 us (3%)
    pallas_call x1, Pallas kernels, per_device(): pl.pallas_call(functools.partial(kernel, n_seq, n_head), out_shape=(pltpu...  47.8 us
    pallas_call x1, Pallas kernels, per_device(): pl.pallas_call(store_kernel, out_shape=tuple((jax.ShapeDtypeStruct(r.shap...  1.38 us

profile of v3, /device:TPU:27, one launch (start us, length us, event | category | flops | bytes accessed | tf_op | source)
XLA Modules:
  0.0 50.5 jit_solution(11502181150187653412)
XLA Ops:
  1.3 47.8 %shard_map.121 = (bf16[1,256,4096]{2,1,0:T(8,128)(2,1)S(1)}, bf16[2,2,128]{2,1,0:T(2,128)(2,1)S(1)}, f32[2,128,128]{2,1,0:T(8,128)S(1)}) custom-call(s32[1]{0:T(128)S(6)} %copy.13.len_ref, bf16[1,256,4096]{2,1,0:T(8,128)(2,1)} %q_hbm.1, bf16[1,256,4096]{2,1,0:T(8,128)(2,1)} %k_hbm.1, bf16[1,256,4096]{2,1,0:T(8,128)(2,1)} %v_hbm.1, f32[1,32,256]{2,1,0:T(8,128)} %bitcast.1, ...), custom_call_target="tpu_custom_call" | custom-call | tf_op jit(solution)/shard_map/pallas_call | solution.py:401
  49.1 1.4 %shard_map.122 = (bf16[1,256,4096]{2,1,0:T(8,128)(2,1)}, bf16[2,2,128]{2,1,0:T(2,128)(2,1)}, f32[2,128,128]{2,1,0:T(8,128)}) custom-call(bf16[1,256,4096]{2,1,0:T(8,128)(2,1)S(1)} %get-tuple-element.6.refs_0_, bf16[2,2,128]{2,1,0:T(2,128)(2,1)S(1)} %get-tuple-element.7.refs_1_, f32[2,128,128]{2,1,0:T(8,128)S(1)} %get-tuple-element.8.refs_2_), custom_call_target="tpu_custom_call" | custom-call | tf_op jit(solution)/shard_map/pallas_call | solution.py:433
